TPU v7x, 8 devices: a whole 2x2x1 slice. The times are simulated.
8 devices in a mesh: data: 1 (over z), pp: 2 (over y), ep: 4 (over x, core).
Axes of the slice: x: 2, y: 2, z: 1, core: 2. Of those that a mesh axis runs over, the one named last changes fastest.
Arguments:
- O: bfloat16 [2, 6, 128, 64, 4096], P(('data', 'pp'), None, 'ep')
- idx: int32 [2, 6, 4, 128, 8], P(('data', 'pp'), None, 'ep')
- slot: int32 [2, 6, 4, 128, 8], P(('data', 'pp'), None, 'ep')
- g: float32 [2, 6, 4, 128, 8], P(('data', 'pp'), None, 'ep')
- H: bfloat16 [2, 6, 4, 128, 4096], P(('data', 'pp'), None, 'ep')
- w: float32 [2, 4096], P('pp')
- Wq: bfloat16 [2, 4096, 64, 128], P('pp')
- Wk: bfloat16 [2, 4096, 64, 128], P('pp')
- Wv: bfloat16 [2, 4096, 64, 128], P('pp')
- Wo: bfloat16 [2, 64, 128, 4096], P('pp')
Outputs:
- output: bfloat16 [2, 6, 4, 128, 4096], P(('data', 'pp'), None, 'ep')
All inputs are finite; a program needn't handle non-finite values.
Results may differ from a plain program's by a relative error of at most 0.0127664.
Values are sent between devices in bfloat16 or wider.
A program may use at most 1.5 GiB of HBM per device.

v0:
```python
import jax
import jax.numpy as jnp
from jax import lax
from jax.sharding import PartitionSpec as P

EPS = 1e-6


def head_attn(a):
    qh, kh, vh = a
    n = qh.shape[-2]
    s = jnp.einsum('...qe,...ke->...qk', qh, kh, preferred_element_type=jnp.float32) * (qh.shape[-1] ** -0.5)
    r = lax.broadcasted_iota(jnp.int32, (n, n), 0)
    c = lax.broadcasted_iota(jnp.int32, (n, n), 1)
    p = jax.nn.softmax(jnp.where(r >= c, s, -1e30), axis=-1)
    return jnp.einsum('...qk,...ke->...qe', p, vh, preferred_element_type=jnp.float32).astype(jnp.bfloat16)


def layer(y, wn, wq, wk, wv, wo):
    yf = y.astype(jnp.float32)
    x = (yf * lax.rsqrt(jnp.mean(yf * yf, axis=-1, keepdims=True) + EPS) * wn).astype(jnp.bfloat16)
    q = jnp.einsum('tme,eif->itmf', x, wq, preferred_element_type=jnp.float32).astype(jnp.bfloat16)
    k = jnp.einsum('tme,eif->itmf', x, wk, preferred_element_type=jnp.float32).astype(jnp.bfloat16)
    v = jnp.einsum('tme,eif->itmf', x, wv, preferred_element_type=jnp.float32).astype(jnp.bfloat16)
    o = lax.map(head_attn, (q, k, v))
    a = jnp.einsum('itmf,ife->tme', o, wo, preferred_element_type=jnp.float32).astype(jnp.bfloat16)
    return (yf + a.astype(jnp.float32)).astype(jnp.bfloat16)


def solution(mesh):
    npp = mesh.shape['pp']
    nep = mesh.shape['ep']
    perm = [(i, (i + 1) % npp) for i in range(npp)]
    tok = P(('data', 'pp'), None, 'ep', None, None)
    wsp = P('pp', None, None, None)

    def body(O, idx, slot, g, H, w, Wq, Wk, Wv, Wo):
        o = O[0]
        mb, cap, d = o.shape[0], o.shape[2], o.shape[3]
        cg = cap // nep
        recv = lax.all_to_all(o, 'ep', 2, 1, tiled=True)
        ne = recv.shape[1]
        flat = recv.reshape(mb, ne * cg, d)
        ix, sl, gt = idx[0], slot[0], g[0]
        off = lax.axis_index('ep') * cg
        col = jnp.arange(ne * cg, dtype=jnp.int32)
        acc = H[0].astype(jnp.float32)
        for kk in range(ix.shape[-1]):
            s = sl[..., kk]
            pos = jnp.where(s >= 0, ix[..., kk] * cg + s - off, -1)
            sel = (pos[..., None] == col).astype(jnp.bfloat16)
            rows = jnp.einsum('mslr,mrd->msld', sel, flat, preferred_element_type=jnp.float32)
            acc = acc + gt[..., kk, None] * rows
        y = lax.ppermute(acc.astype(jnp.bfloat16), 'pp', perm)
        z = lax.map(lambda yy: layer(yy, w[0], Wq[0], Wk[0], Wv[0], Wo[0]), y)
        return z[None]

    return jax.shard_map(body, mesh=mesh,
                         in_specs=(tok, tok, tok, tok, tok, P('pp', None), wsp, wsp, wsp, wsp),
                         out_specs=tok, check_vma=False)
```

profile of v0, /device:TPU:0, one launch (start us, length us, event | category | flops | bytes accessed | tf_op | source)
XLA Modules:
  0.0 3330.0 jit_solution(11968934896874344208)
XLA Ops:
  0.0 82.4 %copy.63 = bf16[1,6,32,64,4096]{4,2,1,3,0:T(8,128)(2,1)} copy(bf16[1,6,32,64,4096]{4,3,2,1,0:T(8,128)(2,1)} %param.14) | data formatting | bytes 201326592 | tf_op args[0]
  82.5 19.4 all-to-all-start
  106.1 1078.3 %all-to-all-done = bf16[6,32,64,4096]{3,1,0,2:T(8,128)(2,1)} async-done(((bf16[6,32,64,4096]{3,1,0,2:T(8,128)(2,1)}), bf16[6,32,64,4096]{3,1,0,2:T(8,128)(2,1)}, u32[]{:S(2)}, u32[]{:S(2)}) %all-to-all-start) | async-done | bytes 100663328 | tf_op jit(solution)/shard_map/all_to_all | solution.py:41
  1184.5 82.9 %copy.25 = bf16[6,32,4,16,4096]{4,3,1,2,0:T(8,128)(2,1)} copy(bf16[6,32,4,16,4096]{4,1,0,3,2:T(8,128)(2,1)} %bitcast.34) | data formatting | bytes 201326592 | tf_op jit(solution)/shard_map/all_to_all | solution.py:41
  1267.4 37.5 %fusion.66 = f32[6,128,4096]{2,1,0:T(8,128)} fusion(bf16[6,2048,4096]{2,1,0:T(8,128)(2,1)} %bitcast.36, s32[6,128]{1,0:T(8,128)S(1)} %get-tuple-element.152), kind=kOutput, calls=%fused_computation.64 | convolution fusion | flops 12886474752 | bytes 113249280 | tf_op jit(solution)/shard_map/mslr,mrd->msld/dot_general | solution.py:52
  1304.8 37.4 %fusion.67 = f32[6,128,4096]{2,1,0:T(8,128)} fusion(bf16[6,2048,4096]{2,1,0:T(8,128)(2,1)} %bitcast.36, s32[6,128]{1,0:T(8,128)S(1)} %get-tuple-element.151), kind=kOutput, calls=%fused_computation.65 | convolution fusion | flops 12886474752 | bytes 113249280 | tf_op jit(solution)/shard_map/mslr,mrd->msld/dot_general | solution.py:52
  1342.3 37.6 %fusion.68 = f32[6,128,4096]{2,1,0:T(8,128)} fusion(bf16[6,2048,4096]{2,1,0:T(8,128)(2,1)} %bitcast.36, s32[6,128]{1,0:T(8,128)S(1)} %copy-done.2), kind=kOutput, calls=%fused_computation.66 | convolution fusion | flops 12886474752 | bytes 113249280 | tf_op jit(solution)/shard_map/mslr,mrd->msld/dot_general | solution.py:52
  1379.9 37.6 %fusion.69 = f32[6,128,4096]{2,1,0:T(8,128)} fusion(bf16[6,2048,4096]{2,1,0:T(8,128)(2,1)} %bitcast.36, s32[6,128]{1,0:T(8,128)S(1)} %copy-done), kind=kOutput, calls=%fused_computation.67 | convolution fusion | flops 12886474752 | bytes 113249280 | tf_op jit(solution)/shard_map/mslr,mrd->msld/dot_general | solution.py:52
  1417.5 37.4 %fusion.70 = f32[6,128,4096]{2,1,0:T(8,128)} fusion(bf16[6,2048,4096]{2,1,0:T(8,128)(2,1)} %bitcast.36, s32[6,128]{1,0:T(8,128)S(1)} %copy-done.3), kind=kOutput, calls=%fused_computation.68 | convolution fusion | flops 12886474752 | bytes 113249280 | tf_op jit(solution)/shard_map/mslr,mrd->msld/dot_general | solution.py:52
  1454.9 37.4 %fusion.71 = f32[6,128,4096]{2,1,0:T(8,128)} fusion(bf16[6,2048,4096]{2,1,0:T(8,128)(2,1)} %bitcast.36, s32[6,128]{1,0:T(8,128)S(1)} %copy-done.1), kind=kOutput, calls=%fused_computation.69 | convolution fusion | flops 12886474752 | bytes 113249280 | tf_op jit(solution)/shard_map/mslr,mrd->msld/dot_general | solution.py:52
  1492.3 37.5 %fusion.72 = f32[6,128,4096]{2,1,0:T(8,128)} fusion(bf16[6,2048,4096]{2,1,0:T(8,128)(2,1)} %bitcast.36, s32[6,128]{1,0:T(8,128)S(1)} %copy-done.5), kind=kOutput, calls=%fused_computation.70 | convolution fusion | flops 12886474752 | bytes 113249280 | tf_op jit(solution)/shard_map/mslr,mrd->msld/dot_general | solution.py:52
  1529.9 37.7 %fusion.73 = f32[6,128,4096]{2,1,0:T(8,128)} fusion(bf16[6,2048,4096]{2,1,0:T(8,128)(2,1)} %bitcast.36, s32[6,128]{1,0:T(8,128)S(1)} %copy-done.4), kind=kOutput, calls=%fused_computation.71 | convolution fusion | flops 12886474752 | bytes 113249280 | tf_op jit(solution)/shard_map/mslr,mrd->msld/dot_general | solution.py:52
  1567.6 38.3 %fusion.74 = bf16[6,1,128,4096]{3,2,0,1:T(8,128)(2,1)} fusion(f32[6,128,4096]{2,1,0:T(8,128)} %fusion.73, f32[6,128]{1,0:T(8,128)S(1)} %copy-done.10, f32[6,128,4096]{2,1,0:T(8,128)} %fusion.72, f32[6,128]{1,0:T(8,128)S(1)} %copy-done.11, f32[6,128,4096]{2,1,0:T(8,128)} %fusion.71, f32[6,128]{1,0:T(8,128)S(1)} %copy-done.12, f32[6,128,4096]{2,1,0:T(8,128)} %fusion.70, ...), kind=kLoop, calls=%fused_computation.72 | loop fusion | flops 56623104 | bytes 113270784 | tf_op jit(solution)/shard_map/convert_element_type | solution.py:54
  1605.9 2.3 collective-permute-start
  1608.1 45.2 %copy.27 = bf16[1,4096,64,128]{3,1,2,0:T(8,128)(2,1)} copy(bf16[1,4096,64,128]{3,2,1,0:T(8,128)(2,1)} %param.20) | data formatting | bytes 134217728 | tf_op jit(solution)/shard_map/while | solution.py:55
  1653.4 45.3 %copy.28 = bf16[1,4096,64,128]{3,1,2,0:T(8,128)(2,1)} copy(bf16[1,4096,64,128]{3,2,1,0:T(8,128)(2,1)} %param.21) | data formatting | bytes 134217728 | tf_op jit(solution)/shard_map/while | solution.py:55
  1698.6 45.2 %copy.29 = bf16[1,4096,64,128]{3,1,2,0:T(8,128)(2,1)} copy(bf16[1,4096,64,128]{3,2,1,0:T(8,128)(2,1)} %param.22) | data formatting | bytes 134217728 | tf_op jit(solution)/shard_map/while | solution.py:55
  1743.9 1585.8 %while.21 = (s32[]{:T(128)}, bf16[6,1,128,4096]{3,2,1,0:T(8,128)(2,1)}, bf16[6,1,128,4096]{3,2,1,0:T(8,128)(2,1)}, f32[1,4096]{1,0:T(1,128)S(1)}, bf16[1,4096,64...) while((s32[]{:T(128)}, ...), condition=%wide.region_6.7_spmd, body=%wide.region_0.6_spmd.sunk | while | flops 34381905920 | bytes 283502304 | solution.py:55
  1745.7 23.9 convert_bitcast_fusion.7
  1769.6 25.3 convert_bitcast_fusion.8
  1794.9 25.2 convert_bitcast_fusion.9
  1820.1 162.6 %while.22 = (s32[]{:T(128)}, bf16[64,1,128,128]{3,2,1,0:T(8,128)(2,1)}, bf16[64,1,128,128]{3,2,1,0:T(8,128)(2,1)S(1)}, bf16[64,1,128,128]{3,2,1,0:T(8,128)(2,1)}, bf16[64,1,128,128]{3,2,1,0:T(8,128)(2,1)}, /*index=5*/s32[]{:T(128)}) while((s32[]{:T(128)}, bf16[64,1,128,128]{3,2,1,0:T(8,128)(2,1)}, bf16[64,1,128,128]{3,2,1,0:T(8,128)(2,1)S(1)}, ...), condition=%wide.region_5.5_spmd, body=%wide.region_2.4_spmd.sunk | while | flops 8535810 | bytes 332357 | solution.py:25
  1982.7 25.6 fusion.125
  2009.9 24.0 convert_bitcast_fusion.7
  2033.9 25.3 convert_bitcast_fusion.8
  2059.1 25.2 convert_bitcast_fusion.9
  2084.4 162.6 %while.22 = (s32[]{:T(128)}, bf16[64,1,128,128]{3,2,1,0:T(8,128)(2,1)}, bf16[64,1,128,128]{3,2,1,0:T(8,128)(2,1)S(1)}, bf16[64,1,128,128]{3,2,1,0:T(8,128)(2,1)}, bf16[64,1,128,128]{3,2,1,0:T(8,128)(2,1)}, /*index=5*/s32[]{:T(128)}) while((s32[]{:T(128)}, bf16[64,1,128,128]{3,2,1,0:T(8,128)(2,1)}, bf16[64,1,128,128]{3,2,1,0:T(8,128)(2,1)S(1)}, ...), condition=%wide.region_5.5_spmd, body=%wide.region_2.4_spmd.sunk | while | flops 8535810 | bytes 332357 | solution.py:25
  2247.0 25.6 fusion.125
  2274.1 24.0 convert_bitcast_fusion.7
  2298.2 25.3 convert_bitcast_fusion.8
  2323.5 25.2 convert_bitcast_fusion.9
  2348.7 162.6 %while.22 = (s32[]{:T(128)}, bf16[64,1,128,128]{3,2,1,0:T(8,128)(2,1)}, bf16[64,1,128,128]{3,2,1,0:T(8,128)(2,1)S(1)}, bf16[64,1,128,128]{3,2,1,0:T(8,128)(2,1)}, bf16[64,1,128,128]{3,2,1,0:T(8,128)(2,1)}, /*index=5*/s32[]{:T(128)}) while((s32[]{:T(128)}, bf16[64,1,128,128]{3,2,1,0:T(8,128)(2,1)}, bf16[64,1,128,128]{3,2,1,0:T(8,128)(2,1)S(1)}, ...), condition=%wide.region_5.5_spmd, body=%wide.region_2.4_spmd.sunk | while | flops 8535810 | bytes 332357 | solution.py:25
  2511.3 25.6 fusion.125
  2538.4 23.9 convert_bitcast_fusion.7
  2562.3 25.3 convert_bitcast_fusion.8
  2587.6 25.2 convert_bitcast_fusion.9
  2612.8 162.6 %while.22 = (s32[]{:T(128)}, bf16[64,1,128,128]{3,2,1,0:T(8,128)(2,1)}, bf16[64,1,128,128]{3,2,1,0:T(8,128)(2,1)S(1)}, bf16[64,1,128,128]{3,2,1,0:T(8,128)(2,1)}, bf16[64,1,128,128]{3,2,1,0:T(8,128)(2,1)}, /*index=5*/s32[]{:T(128)}) while((s32[]{:T(128)}, bf16[64,1,128,128]{3,2,1,0:T(8,128)(2,1)}, bf16[64,1,128,128]{3,2,1,0:T(8,128)(2,1)S(1)}, ...), condition=%wide.region_5.5_spmd, body=%wide.region_2.4_spmd.sunk | while | flops 8535810 | bytes 332357 | solution.py:25
  2775.5 25.6 fusion.125
  2802.6 24.1 convert_bitcast_fusion.7
  2826.7 25.3 convert_bitcast_fusion.8
  2852.0 25.2 convert_bitcast_fusion.9
  2877.2 162.6 %while.22 = (s32[]{:T(128)}, bf16[64,1,128,128]{3,2,1,0:T(8,128)(2,1)}, bf16[64,1,128,128]{3,2,1,0:T(8,128)(2,1)S(1)}, bf16[64,1,128,128]{3,2,1,0:T(8,128)(2,1)}, bf16[64,1,128,128]{3,2,1,0:T(8,128)(2,1)}, /*index=5*/s32[]{:T(128)}) while((s32[]{:T(128)}, bf16[64,1,128,128]{3,2,1,0:T(8,128)(2,1)}, bf16[64,1,128,128]{3,2,1,0:T(8,128)(2,1)S(1)}, ...), condition=%wide.region_5.5_spmd, body=%wide.region_2.4_spmd.sunk | while | flops 8535810 | bytes 332357 | solution.py:25
  3039.8 25.6 fusion.125
  3067.0 24.0 convert_bitcast_fusion.7
  3091.0 25.3 convert_bitcast_fusion.8
  3116.3 25.2 convert_bitcast_fusion.9
  3141.5 162.6 %while.22 = (s32[]{:T(128)}, bf16[64,1,128,128]{3,2,1,0:T(8,128)(2,1)}, bf16[64,1,128,128]{3,2,1,0:T(8,128)(2,1)S(1)}, bf16[64,1,128,128]{3,2,1,0:T(8,128)(2,1)}, bf16[64,1,128,128]{3,2,1,0:T(8,128)(2,1)}, /*index=5*/s32[]{:T(128)}) while((s32[]{:T(128)}, bf16[64,1,128,128]{3,2,1,0:T(8,128)(2,1)}, bf16[64,1,128,128]{3,2,1,0:T(8,128)(2,1)S(1)}, ...), condition=%wide.region_5.5_spmd, body=%wide.region_2.4_spmd.sunk | while | flops 8535810 | bytes 332357 | solution.py:25
  3304.1 25.6 fusion.125
  (1218 shorter events, 988.8 us)
Async XLA Ops:
  82.4 19.4 copy-start.8
  82.4 19.4 copy-start.9
  82.5 21.3 copy-start.7
  82.5 1102.0 %all-to-all-start = ((bf16[6,32,64,4096]{3,1,0,2:T(8,128)(2,1)}), bf16[6,32,64,4096]{3,1,0,2:T(8,128)(2,1)}, u32[]{:S(2)}, u32[]{:S(2)}) async-start(bf16[6,32,64,4096]{3,1,0,2:T(8,128)(2,1)} %bitcast.166), calls=%async_computation | async-start | bytes 201326592 | tf_op jit(solution)/shard_map/all_to_all | solution.py:41
  1304.8 37.5 %copy-start.2 = (s32[6,128]{1,0:T(8,128)S(1)}, s32[6,128]{1,0:T(8,128)}, u32[]{:S(2)}) copy-start(s32[6,128]{1,0:T(8,128)} %get-tuple-element.150) | copy-start | bytes 9220
  1342.3 37.6 %copy-start = (s32[6,128]{1,0:T(8,128)S(1)}, s32[6,128]{1,0:T(8,128)}, u32[]{:S(2)}) copy-start(s32[6,128]{1,0:T(8,128)} %get-tuple-element.149) | copy-start | bytes 9220
  1379.9 37.6 %copy-start.3 = (s32[6,128]{1,0:T(8,128)S(1)}, s32[6,128]{1,0:T(8,128)}, u32[]{:S(2)}) copy-start(s32[6,128]{1,0:T(8,128)} %get-tuple-element.148) | copy-start | bytes 9220
  1417.5 37.4 %copy-start.1 = (s32[6,128]{1,0:T(8,128)S(1)}, s32[6,128]{1,0:T(8,128)}, u32[]{:S(2)}) copy-start(s32[6,128]{1,0:T(8,128)} %get-tuple-element.147) | copy-start | bytes 9220
  1454.9 37.5 %copy-start.5 = (s32[6,128]{1,0:T(8,128)S(1)}, s32[6,128]{1,0:T(8,128)}, u32[]{:S(2)}) copy-start(s32[6,128]{1,0:T(8,128)} %get-tuple-element.146) | copy-start | bytes 9220
  1492.3 37.5 %copy-start.4 = (s32[6,128]{1,0:T(8,128)S(1)}, s32[6,128]{1,0:T(8,128)}, u32[]{:S(2)}) copy-start(s32[6,128]{1,0:T(8,128)} %get-tuple-element.145) | copy-start | bytes 9220
  1529.8 37.7 %copy-start.10 = (f32[6,128]{1,0:T(8,128)S(1)}, f32[6,128]{1,0:T(8,128)}, u32[]{:S(2)}) copy-start(f32[6,128]{1,0:T(8,128)} %get-tuple-element.153) | copy-start | bytes 9220
  1529.8 37.7 %copy-start.11 = (f32[6,128]{1,0:T(8,128)S(1)}, f32[6,128]{1,0:T(8,128)}, u32[]{:S(2)}) copy-start(f32[6,128]{1,0:T(8,128)} %get-tuple-element.154) | copy-start | bytes 9220
  1529.8 37.7 %copy-start.12 = (f32[6,128]{1,0:T(8,128)S(1)}, f32[6,128]{1,0:T(8,128)}, u32[]{:S(2)}) copy-start(f32[6,128]{1,0:T(8,128)} %get-tuple-element.155) | copy-start | bytes 9220
  1529.8 37.7 %copy-start.13 = (f32[6,128]{1,0:T(8,128)S(1)}, f32[6,128]{1,0:T(8,128)}, u32[]{:S(2)}) copy-start(f32[6,128]{1,0:T(8,128)} %get-tuple-element.156) | copy-start | bytes 9220
  1529.8 37.7 %copy-start.14 = (f32[6,128]{1,0:T(8,128)S(1)}, f32[6,128]{1,0:T(8,128)}, u32[]{:S(2)}) copy-start(f32[6,128]{1,0:T(8,128)} %get-tuple-element.157) | copy-start | bytes 9220
  1529.8 37.7 %copy-start.15 = (f32[6,128]{1,0:T(8,128)S(1)}, f32[6,128]{1,0:T(8,128)}, u32[]{:S(2)}) copy-start(f32[6,128]{1,0:T(8,128)} %get-tuple-element.158) | copy-start | bytes 9220
  1529.8 37.7 %copy-start.16 = (f32[6,128]{1,0:T(8,128)S(1)}, f32[6,128]{1,0:T(8,128)}, u32[]{:S(2)}) copy-start(f32[6,128]{1,0:T(8,128)} %get-tuple-element.159) | copy-start | bytes 9220
  1529.8 37.7 %copy-start.17 = (f32[6,128]{1,0:T(8,128)S(1)}, f32[6,128]{1,0:T(8,128)}, u32[]{:S(2)}) copy-start(f32[6,128]{1,0:T(8,128)} %get-tuple-element.160) | copy-start | bytes 9220
  1605.9 138.0 %collective-permute-start = (bf16[6,1,128,4096]{3,2,0,1:T(8,128)(2,1)}, bf16[6,1,128,4096]{3,2,0,1:T(8,128)(2,1)}, u32[]{:S(2)}, u32[]{:S(2)}) collective-permute-start(bf16[6,1,128,4096]{3,2,0,1:T(8,128)(2,1)} %fusion.74), channel_id=1, source_target_pairs={{0,4},{4,0},{1,5},{5,1},{2,6},{6,2},{3,7},{7,3}} | collective-permute-start | bytes 18874376 | tf_op jit(solution)/shard_map/ppermute | solution.py:54
  1698.6 45.3 %copy-start.6 = (f32[1,4096]{1,0:T(1,128)S(1)}, f32[1,4096]{1,0:T(1,128)}, u32[]{:S(2)}) copy-start(f32[1,4096]{1,0:T(1,128)} %param.19) | copy-start | bytes 49156
where the time goes:
time: 3390 us; the launch traced here: 3330 us
  matrix products  1860 us (55%)
  waiting for transfers between devices  1080 us (32%)
  local copies, waits for them, and re-layouts  305 us (9%)
  other arithmetic  64.9 us (2%)
    all_to_all x1, waiting for transfers between devices, body(): recv = lax.all_to_all(o, 'ep', 2, 1, tiled=True)  1080 us
    dot_general x384, matrix products, head_attn(): jnp.einsum('...qk,...ke->...qe', p, vh, preferred_element_type=jnp.float32)  599 us
    dot_general x384, matrix products, head_attn(): jnp.einsum('...qe,...ke->...qk', qh, kh, preferred_element_type=jnp.float32)  359 us
    dot_general x8, matrix products, body(): jnp.einsum('mslr,mrd->msld', sel, flat, preferred_element_type=jnp.float32)  300 us
    dot_general x6, matrix products, layer(): jnp.einsum('itmf,ife->tme', o, wo, preferred_element_type=jnp.float32)  154 us
    dot_general x6, matrix products, layer(): jnp.einsum('tme,eif->itmf', x, wk, preferred_element_type=jnp.float32)  152 us
    dot_general x6, matrix products, layer(): jnp.einsum('tme,eif->itmf', x, wv, preferred_element_type=jnp.float32)  151 us
    dot_general x6, matrix products, layer(): jnp.einsum('tme,eif->itmf', x, wq, preferred_element_type=jnp.float32)  144 us
  transfers between devices with their start and end apart: 2, of which 1 were waited for; matrix products, arithmetic and copies ran while one was open for 4% of the time, Pallas kernels for 0%

commit v1 on v0

v1 whole, which is shorter than its diff:
```python
import functools
import jax
import jax.numpy as jnp
from jax import lax
from jax.experimental import pallas as pl
from jax.experimental.pallas import tpu as pltpu
from jax.sharding import PartitionSpec as P

EPS = 1e-6
F32, BF16 = jnp.float32, jnp.bfloat16
VMEM_LIMIT = 58 * 1024 * 1024


def params(n):
    return pltpu.CompilerParams(dimension_semantics=("arbitrary",) * n, vmem_limit_bytes=VMEM_LIMIT)


def partial_kernel(cg, nout, has_add, sp, r_ref, o_ref, *rest):
    out_refs, g_ref = rest[-1 - nout:-1], rest[-1]
    ne, _, d = o_ref.shape[1:]
    n, rows = r_ref.shape[2], ne * cg
    q = lax.broadcasted_iota(jnp.int32, (n, rows), 1)
    code = (sp[0] * (ne * cg * 4) + (q // cg) * (cg * 4) + sp[1] * cg + q % cg).astype(F32)
    r = r_ref[0, 0]
    top = r.shape[1] // 2
    gm = jnp.zeros((n, rows), F32)
    for k in range(top):
        gm = jnp.where(r[:, k:k + 1] == code, r[:, top + k:top + k + 1], gm)
    hi = gm.astype(BF16)
    g_ref[0:n] = hi
    r1 = gm - hi.astype(F32)
    mid = r1.astype(BF16)
    g_ref[n:2 * n] = mid
    g_ref[2 * n:] = (r1 - mid.astype(F32)).astype(BF16)
    acc = jnp.dot(g_ref[...], o_ref[0].reshape(rows, d), preferred_element_type=F32)
    s = acc[0:n] + acc[n:2 * n] + acc[2 * n:]
    if has_add:
        s = s + rest[0][0]
    if nout == 1:
        out_refs[0][0] = s
        return
    for i, out_ref in enumerate(out_refs):
        @pl.when(pl.program_id(0) == i)
        def _():
            out_ref[0] = s


def partials(m0, nm, sp, routes, o, add=None, add_at=0, split=False):
    nout = nm if split else 1
    _, ne, cap, d = o.shape
    n, cg = routes.shape[2], cap // 4
    in_specs = [
        pl.BlockSpec((1, 1, n, routes.shape[3]), lambda i, sp: (sp[1], m0 + i, 0, 0)),
        pl.BlockSpec((1, ne, cg, d), lambda i, sp: (m0 + i, 0, sp[1], 0)),
    ]
    ops = [routes, o]
    if add is not None:
        in_specs.append(pl.BlockSpec((1, n, d), lambda i, sp: (add_at + i, 0, 0)))
        ops.append(add)
    return pl.pallas_call(
        functools.partial(partial_kernel, cg, nout, add is not None),
        grid_spec=pltpu.PrefetchScalarGridSpec(
            num_scalar_prefetch=1, grid=(nm,), in_specs=in_specs,
            out_specs=[pl.BlockSpec((1, n, d), lambda i, sp: (0 if split else i, 0, 0))] * nout,
            scratch_shapes=[pltpu.VMEM((3 * n, ne * cg), BF16)]),
        out_shape=[jax.ShapeDtypeStruct((nm // nout, n, d), F32)] * nout,
        compiler_params=params(1), name="partials",
        cost_estimate=pl.CostEstimate(flops=nm * 6 * n * ne * cg * d, transcendentals=0,
                                      bytes_accessed=nm * (ne * cg * d * 2 + n * d * 4)),
    )(sp, *ops)


def relayout_kernel(sp, w_ref, o_ref, s_ref):
    eb, nh = w_ref.shape[1:3]
    for j in range(nh // 8):
        s_ref[...] = w_ref[0, :, j * 8:j * 8 + 8, :].astype(F32).reshape(eb * 8, 128)
        for i in range(8):
            h = j * 8 + i
            o_ref[h // 2, :, (h % 2) * 128:(h % 2) * 128 + 128] = s_ref[pl.ds(i, eb, stride=8), :].astype(BF16)


def relayout(sp, w, eb=512, hb=16):
    _, e, h, f = w.shape
    return pl.pallas_call(
        relayout_kernel,
        grid_spec=pltpu.PrefetchScalarGridSpec(
            num_scalar_prefetch=1, grid=(e // eb, h // 2 // hb),
            in_specs=[pl.BlockSpec((1, eb, hb, f), lambda i, j, sp: (0, i, sp[0] * (h // 2 // hb) + j, 0))],
            out_specs=pl.BlockSpec((hb // 2, eb, 2 * f), lambda i, j, sp: (j, i, 0)),
            scratch_shapes=[pltpu.VMEM((eb * 8, f), F32)]),
        out_shape=jax.ShapeDtypeStruct((h // 4, e, 2 * f), BF16),
        compiler_params=params(2), name="relayout",
        cost_estimate=pl.CostEstimate(flops=10 ** 9, transcendentals=0, bytes_accessed=e * h * f * 2),
    )(sp, w)


def attention(n, qkv, o_refs):
    hd = qkv.shape[1] // 6
    mask = lax.broadcasted_iota(jnp.int32, (n, n), 0) >= lax.broadcasted_iota(jnp.int32, (n, n), 1)
    ones = jnp.ones((n, hd), BF16)
    tiles = [(t, h) for t in range(qkv.shape[0] // n) for h in range(2)]
    part = lambda t, h, j: qkv[t * n:(t + 1) * n, (2 * j + h) * hd:(2 * j + h + 1) * hd]
    ss = [lax.dot_general(part(t, h, 0), part(t, h, 1), (((1,), (1,)), ((), ())), preferred_element_type=F32)
          for t, h in tiles]
    ps = []
    for s in ss:
        s = jnp.where(mask, s * hd ** -0.5, -1e30)
        ps.append(jnp.exp(s - jnp.max(s, axis=-1, keepdims=True)))
    for (t, h), p in zip(tiles, ps):
        hi = p.astype(BF16)
        lo = (p - hi.astype(F32)).astype(BF16)
        ve = jnp.concatenate([part(t, h, 2), ones], axis=1)
        o = jnp.dot(jnp.concatenate([hi, lo], axis=1), jnp.concatenate([ve, ve], axis=0), preferred_element_type=F32)
        nt = o_refs[0].shape[0] // n
        o_refs[t // nt][(t % nt) * n:(t % nt + 1) * n, h * hd:(h + 1) * hd] = (o[:, :hd] / o[:, hd:]).astype(BF16)


def qkva_kernel(n, nu, *refs):
    u_refs, (g_ref, wq_ref, wk_ref, wv_ref, om_ref, os_ref, x_ref, qkv_ref) = refs[:nu], refs[nu:]

    @pl.when(pl.program_id(0) == 0)
    def _():
        at = 0
        for u_ref in u_refs:
            for r in range(0, u_ref.shape[0], 32):
                u = u_ref[r:r + 32].astype(F32)
                x = u * lax.rsqrt(jnp.mean(u * u, axis=-1, keepdims=True) + EPS) * g_ref[...]
                x_ref[at:at + 32] = x.astype(BF16)
                at += 32

    x = x_ref[...]
    f2 = wq_ref.shape[2]
    for j, w_ref in enumerate((wq_ref, wk_ref, wv_ref)):
        qkv_ref[:, j * f2:(j + 1) * f2] = jnp.dot(x, w_ref[0], preferred_element_type=F32).astype(BF16)
    attention(n, qkv_ref[...], (om_ref, os_ref))


def qkva(n, us, gain, wq, wk, wv):
    t = sum(u.shape[0] for u in us)
    d = us[0].shape[1]
    steps, _, f2 = wq.shape
    res = lambda shape: pl.BlockSpec(shape, lambda i: (0, 0), pipeline_mode=pl.Buffered(1))
    wspec = pl.BlockSpec((1, d, f2), lambda i: (i, 0, 0))
    ospec = pl.BlockSpec((t // 2, f2), lambda i: (0, i))
    osh = jax.ShapeDtypeStruct((t // 2, steps * f2), BF16)
    return pl.pallas_call(
        functools.partial(qkva_kernel, n, len(us)), grid=(steps,),
        in_specs=[res(u.shape) for u in us] + [res(gain.shape), wspec, wspec, wspec],
        out_specs=[ospec, ospec], out_shape=[osh, osh],
        scratch_shapes=[pltpu.VMEM((t, d), BF16), pltpu.VMEM((t, 3 * f2), BF16)],
        compiler_params=params(1), name="qkva",
        cost_estimate=pl.CostEstimate(flops=6 * t * d * steps * f2, transcendentals=0,
                                      bytes_accessed=6 * d * steps * f2),
    )(*us, gain, wq, wk, wv)


def oproj_kernel(nu, sp, am_ref, ar_ref, wm_ref, wr_ref, *rest):
    u_refs, z_ref = rest[:nu], rest[-1]
    acc = jnp.dot(am_ref[...], wm_ref[...], preferred_element_type=F32)
    acc = acc + jnp.dot(ar_ref[...], wr_ref[...], preferred_element_type=F32)
    at = 0
    for u_ref in u_refs:
        r = slice(at, at + u_ref.shape[0])
        z_ref[r] = (u_ref[...].astype(F32) + acc[r].astype(BF16).astype(F32)).astype(BF16)
        at += u_ref.shape[0]


def oproj(gi, total, sp, am, ar, wo, us, z, nt=512):
    t, kh = am.shape
    d = wo.shape[1]
    aspec = pl.BlockSpec((t, kh), lambda i, sp: (0, 0), pipeline_mode=pl.Buffered(1))
    in_specs = [aspec, aspec, pl.BlockSpec((kh, nt), lambda i, sp: (sp[0], i)),
                pl.BlockSpec((kh, nt), lambda i, sp: (1 - sp[0], i))]
    in_specs += [pl.BlockSpec((u.shape[0], nt), lambda i, sp: (0, i)) for u in us]
    ops = [sp, am, ar, wo, wo, *us]
    alias = {}
    if z is not None:
        alias = {len(ops): 0}
        in_specs.append(pl.BlockSpec(memory_space=pl.ANY))
        ops.append(z)
    return pl.pallas_call(
        functools.partial(oproj_kernel, len(us)),
        grid_spec=pltpu.PrefetchScalarGridSpec(
            num_scalar_prefetch=1, grid=(d // nt,), in_specs=in_specs,
            out_specs=pl.BlockSpec((t, nt), lambda i, sp: (gi, i))),
        out_shape=jax.ShapeDtypeStruct((total, d), BF16), input_output_aliases=alias,
        compiler_params=params(1), name="oproj",
        cost_estimate=pl.CostEstimate(flops=4 * t * kh * d, transcendentals=0, bytes_accessed=4 * kh * d),
    )(*ops)


def solution(mesh):
    npp, nep = mesh.shape['pp'], mesh.shape['ep']
    yperm = [(i, (i + 1) % npp) for i in range(npp)]
    cperm = [(i, i ^ 1) for i in range(nep)]
    xperm = [(i, i ^ 2) for i in range(nep)]
    tok = P(('data', 'pp'), None, 'ep', None, None)
    wsp = P('pp', None, None, None)

    def body(O, idx, slot, g, H, w, Wq, Wk, Wv, Wo):
        o, h = O[0], H[0, :, 0]
        mb, n, d = h.shape
        cap = o.shape[2]
        ep = lax.axis_index('ep')
        pos = jnp.where(slot[0, :, 0] >= 0, idx[0, :, 0] * cap + slot[0, :, 0], -1).astype(F32)
        routes = lax.all_gather(jnp.concatenate([pos, g[0, :, 0]], axis=-1), 'ep')
        own = [jnp.stack([ep, ep ^ i]).astype(jnp.int32) for i in range(nep)]
        core = (ep % 2).reshape(1).astype(jnp.int32)
        wo = Wo[0].reshape(-1, d)

        last = [own[0]]

        def run(f, sp, *a, **k):
            sp, _ = lax.optimization_barrier((sp, last[0]))
            out = f(sp, *a, **k)
            last[0] = out[0] if isinstance(out, (list, tuple)) else out
            return out

        def part(m0, nm, k, *a, **kw):
            return run(lambda sp: partials(m0, nm, sp, routes, o, *a, **kw), own[k])

        a01 = lax.ppermute(part(0, 2, 3)[0], 'ep', cperm)
        a25 = lax.ppermute(part(2, 4, 3)[0], 'ep', cperm)
        far = part(0, 2, 2, a01, 0, split=True)
        far = [lax.ppermute(f, 'ep', xperm) for f in far]
        rest = part(2, 4, 2, a25, 0, split=True)
        far += [lax.ppermute(f, 'ep', xperm) for f in rest]
        b = lax.ppermute(part(0, mb, 1)[0], 'ep', cperm)

        def rel(W):
            return run(relayout, core, W)

        wq = rel(Wq)
        near = part(0, mb, 0, b, 0)[0]

        def hop(m):
            near_, _ = lax.optimization_barrier((near[m], last[0]))
            y = (h[m].astype(F32) + near_ + far[m][0]).astype(BF16)
            last[0] = y
            u = lax.ppermute(y, 'pp', yperm)
            return u, lax.ppermute(u, 'ep', cperm)

        def attend(us):
            u = [p[0] for p in us] + [p[1] for p in us]
            u[0], _ = lax.optimization_barrier((u[0], last[0]))
            om, os = qkva(n, u, w, wq, wk, wv)
            last[0] = om
            return om, lax.ppermute(os, 'ep', cperm)

        def project(gi, us, am, ar, z):
            return run(lambda sp: oproj(gi, mb * n, sp, am, ar, wo, [p[0] for p in us], z), core)

        u0 = hop(0)
        u1 = hop(1)
        wk = rel(Wk)
        wv = rel(Wv)
        u2 = hop(2)
        at0 = attend([u0, u1])
        u3 = hop(3)
        z = project(0, [u0, u1], *at0, None)
        u4 = hop(4)
        at1 = attend([u2, u3])
        u5 = hop(5)
        z = project(1, [u2, u3], *at1, z)
        at2 = attend([u4, u5])
        z = project(2, [u4, u5], *at2, z)
        return z.reshape(1, mb, 1, n, d)

    return jax.shard_map(body, mesh=mesh,
                         in_specs=(tok, tok, tok, tok, tok, P('pp', None), wsp, wsp, wsp, wsp),
                         out_specs=tok, check_vma=False)
```

time: 3390 us -> 663 us (0.20); the launches traced: 3330 us -> 653 us
  matrix products: 1860 us -> 0 us
  waiting for transfers between devices: 1080 us -> 92.5 us
  Pallas kernels: 0 us -> 499 us
  local copies, waits for them, and re-layouts: 305 us -> 16.5 us
  other arithmetic: 64.9 us -> 20.3 us
    dot_general x800 -> x0, matrix products: 1860 us -> none  [the longest x384 599 us: head_attn(): jnp.einsum('...qk,...ke->...qe', p, vh, preferred_element_type=jnp.float32)]
    all_to_all x1 -> x0, waiting for transfers between devices: 1080 us -> none  [body(): recv = lax.all_to_all(o, 'ep', 2, 1, tiled=True)]
    pallas_call x0 -> x15, Pallas kernels: none -> 499 us  [the longest x3 218 us: qkva(): pl.pallas_call(functools.partial(qkva_kernel, n, len(us)), grid=(steps,),...]
    while x3 -> x0, local copies, waits for them, and re-layouts: 136 us -> none  [body(): z = lax.map(lambda yy: layer(yy, w[0], Wq[0], Wk[0], Wv[0], Wo[0]), y)]
    ppermute x1 -> x24, waiting for transfers between devices: 0.01 us -> 92.5 us  [the longest x6 46.8 us: hop(): u = lax.ppermute(y, 'pp', yperm)]
    all_to_all x1 -> x0, local copies, waits for them, and re-layouts: 82.9 us -> none  [body(): recv = lax.all_to_all(o, 'ep', 2, 1, tiled=True)]
    unnamed x45 -> x20, local copies, waits for them, and re-layouts: 86.7 us -> 5.97 us
  transfers between devices with their start and end apart: 2 -> 24, of which waited for: 1 -> 5; matrix products, arithmetic and copies ran while one was open for 4% -> 4% of each run, Pallas kernels for 0% -> 52%
where the time goes in v1:
time: 663 us; the launch traced here: 653 us
  Pallas kernels  499 us (75%)
  waiting for transfers between devices  92.5 us (14%)
  other arithmetic  20.3 us (3%)
  local copies, waits for them, and re-layouts  16.5 us (2%)
  starting transfers between devices  13 us (2%)
  blocking collectives  10.5 us (2%)
    pallas_call x3, Pallas kernels, qkva(): pl.pallas_call(functools.partial(qkva_kernel, n, len(us)), grid=(steps,),...  218 us
    pallas_call x3, Pallas kernels, relayout(): pl.pallas_call(relayout_kernel, grid_spec=pltpu.PrefetchScalarGridSpec(nu...  98.2 us
    pallas_call x6, Pallas kernels, partials(): pl.pallas_call(functools.partial(partial_kernel, cg, nout, add is not Non...  92.9 us
    pallas_call x3, Pallas kernels, oproj(): pl.pallas_call(functools.partial(oproj_kernel, len(us)), grid_spec=pltpu....  89.9 us
    ppermute x6, waiting for transfers between devices, hop(): u = lax.ppermute(y, 'pp', yperm)  46.8 us
    ppermute x2, waiting for transfers between devices, body(): far = [lax.ppermute(f, 'ep', xperm) for f in far]  23.9 us
    ppermute x1, waiting for transfers between devices, body(): a01 = lax.ppermute(part(0, 2, 3)[0], 'ep', cperm)  17.7 us
    convert_element_type x6, other arithmetic, hop(): y = (h[m].astype(F32) + near_ + far[m][0]).astype(BF16)  16.9 us
  transfers between devices with their start and end apart: 24, of which 5 were waited for; matrix products, arithmetic and copies ran while one was open for 4% of the time, Pallas kernels for 52%

profile of v1, /device:TPU:0, one launch (start us, length us, event | category | flops | bytes accessed | tf_op | source)
XLA Modules:
  0.0 652.5 jit_solution(14470231086472888544)
XLA Ops:
  0.0 0.6 pad_add_fusion
  0.6 0.8 fusion.15
  1.4 0.7 pad_maximum_fusion
  2.1 10.5 %all-gather = f32[24,128,16]{1,2,0:T(8,128)S(1)} all-gather(f32[6,128,16]{1,2,0:T(8,128)S(1)} %pad_maximum_fusion), channel_id=2, replica_groups=mesh['data'=1,'pp'=2,'ep'=4] {'ep'}, dimensions={0}, use_global_device_ids=true | all-gather | bytes 245760 | tf_op jit(solution)/shard_map/all_gather | solution.py:206
  12.6 1.7 copy.21
  14.3 8.7 %partials.6 = f32[2,128,4096]{2,1,0:T(8,128)} custom-call(s32[2]{0:T(128)} %get-tuple-element.39.sp, f32[4,6,128,16]{3,2,1,0:T(8,128)} %bitcast.71, bf16[6,32,64,4096]{3,2,1,0:T(8,128)(2,1)} %bitcast.11.o_ref), custom_call_target="tpu_custom_call" | custom-call | flops 3221225472 | bytes 12582912 | tf_op jit(solution)/shard_map/partials/pallas_call | solution.py:60
  23.0 14.1 %partials.7 = f32[4,128,4096]{2,1,0:T(8,128)} custom-call(s32[2]{0:T(128)} %get-tuple-element.39.sp, f32[4,6,128,16]{3,2,1,0:T(8,128)} %bitcast.72, bf16[6,32,64,4096]{3,2,1,0:T(8,128)(2,1)} %bitcast.11.o_ref), custom_call_target="tpu_custom_call" | custom-call | flops 6442450944 | bytes 25165824 | tf_op jit(solution)/shard_map/partials/pallas_call | solution.py:60
  37.2 0.5 collective-permute-start
  37.7 0.6 pad_add_fusion.2.sp
  38.3 0.7 pad_add_fusion.1.sp
  38.9 17.7 %collective-permute-done.rest_0_ = f32[2,128,4096]{2,1,0:T(8,128)} collective-permute-done((f32[2,128,4096]{2,1,0:T(8,128)}, f32[2,128,4096]{2,1,0:T(8,128)}, u32[]{:S(2)}, u32[]{:S(2)}) %collective-permute-start) | collective-permute-done | bytes 4194336 | tf_op jit(solution)/shard_map/ppermute | solution.py:222
  56.7 10.4 %partials.8 = (f32[1,128,4096]{2,1,0:T(8,128)}, f32[1,128,4096]{2,1,0:T(8,128)}) custom-call(s32[2]{0:T(128)} %pad_add_fusion.2.sp, f32[4,6,128,16]{3,2,1,0:T(8,128)} %bitcast.73, bf16[6,32,64,4096]{3,2,1,0:T(8,128)(2,1)} %bitcast.11.o_ref, f32[2,128,4096]{2,1,0:T(8,128)} %collective-permute-done.rest_0_), custom_call_target="tpu_custom_call" | custom-call | flops 3221225472 | bytes 12582912 | tf_op jit(solution)/shard_map/partials/pallas_call | solution.py:60
  67.0 16.9 %partials.9 = (f32[1,128,4096]{2,1,0:T(8,128)}, f32[1,128,4096]{2,1,0:T(8,128)}, f32[1,128,4096]{2,1,0:T(8,128)}, f32[1,128,4096]{2,1,0:T(8,128)}) custom-call(s32[2]{0:T(128)} %pad_add_fusion.2.sp, f32[4,6,128,16]{3,2,1,0:T(8,128)} %bitcast.74, bf16[6,32,64,4096]{3,2,1,0:T(8,128)(2,1)} %bitcast.11.o_ref, f32[4,128,4096]{2,1,0:T(8,128)} %collective-permute-done.1.rest_0_), custom_call_target="tpu_custom_call" | custom-call | flops 6442450944 | bytes 25165824 | tf_op jit(solution)/shard_map/partials/pallas_call | solution.py:60
  84.0 19.6 %partials.10 = f32[6,128,4096]{2,1,0:T(8,128)} custom-call(s32[2]{0:T(128)} %pad_add_fusion.1.sp, f32[4,6,128,16]{3,2,1,0:T(8,128)} %bitcast.75, bf16[6,32,64,4096]{3,2,1,0:T(8,128)(2,1)} %bitcast.11.o_ref), custom_call_target="tpu_custom_call" | custom-call | flops 9663676416 | bytes 37748736 | tf_op jit(solution)/shard_map/partials/pallas_call | solution.py:60
  103.7 2.0 collective-permute-start.5
  105.8 32.7 %relayout.3.refs_5_ = bf16[16,4096,256]{2,1,0:T(8,128)(2,1)} custom-call(s32[1]{0:T(128)} %bitcast.sp, bf16[1,4096,64,128]{3,2,1,0:T(8,128)(2,1)} %w_ref.3), custom_call_target="tpu_custom_call" | custom-call | flops 1000000000 | bytes 67108864 | tf_op jit(solution)/shard_map/relayout/pallas_call | solution.py:84
  138.5 23.2 %partials.11 = f32[6,128,4096]{2,1,0:T(8,128)} custom-call(s32[2]{0:T(128)} %get-tuple-element.46.sp, f32[4,6,128,16]{3,2,1,0:T(8,128)} %bitcast.76, bf16[6,32,64,4096]{3,2,1,0:T(8,128)(2,1)} %bitcast.11.o_ref, f32[6,128,4096]{2,1,0:T(8,128)} %collective-permute-done.2.rest_0_), custom_call_target="tpu_custom_call" | custom-call | flops 9663676416 | bytes 37748736 | tf_op jit(solution)/shard_map/partials/pallas_call | solution.py:60
  161.8 8.8 %slice_bitcast_fusion = (f32[128,4096]{1,0:T(8,128)}, f32[128,4096]{1,0:T(8,128)}, f32[128,4096]{1,0:T(8,128)S(1)}, f32[128,4096]{1,0:T(8,128)}, f32[128,4096]{1,0:T(8,128)S(1)}, /*index=5*/f32[128,4096]{1,0:T(8,128)}) fusion(f32[6,128,4096]{2,1,0:T(8,128)} %partials.11), kind=kLoop, calls=%fused_computation | loop fusion | bytes 25165824 | tf_op jit(solution)/shard_map/squeeze | solution.py:237
  170.6 3.0 fusion.7
  173.6 23.9 %collective-permute-done.5 = f32[1,128,4096]{2,1,0:T(8,128)} collective-permute-done((f32[1,128,4096]{2,1,0:T(8,128)}, f32[1,128,4096]{2,1,0:T(8,128)}, u32[]{:S(2)}, u32[]{:S(2)}) %collective-permute-start.5) | collective-permute-done | bytes 2097184 | tf_op jit(solution)/shard_map/ppermute | solution.py:225
  197.4 3.2 fusion.3
  200.7 1.5 collective-permute-start.7
  202.8 32.7 %relayout.4.refs_6_ = bf16[16,4096,256]{2,1,0:T(8,128)(2,1)} custom-call(s32[1]{0:T(128)} %bitcast.sp, bf16[1,4096,64,128]{3,2,1,0:T(8,128)(2,1)} %w_ref.4), custom_call_target="tpu_custom_call" | custom-call | flops 1000000000 | bytes 67108864 | tf_op jit(solution)/shard_map/relayout/pallas_call | solution.py:84
  235.5 32.8 %relayout.5.refs_7_ = bf16[16,4096,256]{2,1,0:T(8,128)(2,1)} custom-call(s32[1]{0:T(128)} %bitcast.sp, bf16[1,4096,64,128]{3,2,1,0:T(8,128)(2,1)} %w_ref.5), custom_call_target="tpu_custom_call" | custom-call | flops 1000000000 | bytes 67108864 | tf_op jit(solution)/shard_map/relayout/pallas_call | solution.py:84
  268.8 3.2 fusion.5
  271.9 2.0 collective-permute-start.14
  273.9 72.7 %qkva.3 = (bf16[256,4096]{1,0:T(8,128)(2,1)}, bf16[256,4096]{1,0:T(8,128)(2,1)}) custom-call(bf16[128,4096]{1,0:T(8,128)(2,1)} %collective-permute-done.4.refs_0_.rest_0_, bf16[128,4096]{1,0:T(8,128)(2,1)} %collective-permute-done.7.refs_1_.rest_1_, bf16[128,4096]{1,0:T(8,128)(2,1)} %collective-permute-done.8.refs_2_, ...), custom_call_target="tpu_custom_call" | custom-call | flops 51539607552 | bytes 100663296 | tf_op jit(solution)/shard_map/qkva/pallas_call | solution.py:146
  346.6 2.2 fusion.9
  348.8 0.9 collective-permute-start.15
  349.8 1.5 collective-permute-start.12
  351.3 0.5 collective-permute-start.18
  351.8 22.7 %collective-permute-done.15.refs_1_.rest_1_ = bf16[128,4096]{1,0:T(8,128)(2,1)} collective-permute-done((bf16[128,4096]{1,0:T(8,128)(2,1)S(1)}, bf16[128,4096]{1,0:T(8,128)(2,1)}, u32[]{:S(2)}, u32[]{:S(2)}) %collective-permute-start.15) | collective-permute-done | bytes 1048608 | tf_op jit(solution)/shard_map/ppermute | solution.py:240
  374.5 1.3 copy-done.3
  375.9 30.1 %oproj.3.rest_2_ = bf16[768,4096]{1,0:T(8,128)(2,1)} custom-call(s32[1]{0:T(128)} %bitcast.sp, bf16[256,4096]{1,0:T(8,128)(2,1)} %get-tuple-element.54.am_ref, bf16[256,4096]{1,0:T(8,128)(2,1)} %copy-done.3, bf16[8192,4096]{1,0:T(8,128)(2,1)} %bitcast.25.wm_ref.wr_ref, bf16[8192,4096]{1,0:T(8,128)(2,1)} %bitcast.25.wm_ref.wr_ref, ...), custom_call_target="tpu_custom_call" | custom-call | flops 17179869184 | bytes 67108864 | tf_op jit(solution)/shard_map/oproj/pallas_call | solution.py:181
  406.0 3.2 fusion.11
  409.2 0.8 collective-permute-start.13
  410.0 72.7 %qkva.4 = (bf16[256,4096]{1,0:T(8,128)(2,1)}, bf16[256,4096]{1,0:T(8,128)(2,1)}) custom-call(bf16[128,4096]{1,0:T(8,128)(2,1)} %copy-done.6, bf16[128,4096]{1,0:T(8,128)(2,1)} %collective-permute-done.15.refs_1_.rest_1_, bf16[128,4096]{1,0:T(8,128)(2,1)} %collective-permute-done.16.refs_2_, bf16[128,4096]{1,0:T(8,128)(2,1)} %collective-permute-done.17.refs_3_, ...), custom_call_target="tpu_custom_call" | custom-call | flops 51539607552 | bytes 100663296 | tf_op jit(solution)/shard_map/qkva/pallas_call | solution.py:146
  483.1 2.2 fusion.1
  485.3 1.2 collective-permute-start.20
  486.4 24.1 %collective-permute-done.20.refs_1_.rest_1_ = bf16[128,4096]{1,0:T(8,128)(2,1)S(1)} collective-permute-done((bf16[128,4096]{1,0:T(8,128)(2,1)S(1)}, bf16[128,4096]{1,0:T(8,128)(2,1)S(1)}, u32[]{:S(2)}, u32[]{:S(2)}) %collective-permute-start.20) | collective-permute-done | bytes 1048608 | tf_op jit(solution)/shard_map/ppermute | solution.py:240
  510.5 1.3 copy-done.4
  511.9 29.9 %oproj.4.rest_2_ = bf16[768,4096]{1,0:T(8,128)(2,1)} custom-call(s32[1]{0:T(128)} %bitcast.sp, bf16[256,4096]{1,0:T(8,128)(2,1)} %get-tuple-element.62.am_ref, bf16[256,4096]{1,0:T(8,128)(2,1)} %copy-done.4, bf16[8192,4096]{1,0:T(8,128)(2,1)} %bitcast.25.wm_ref.wr_ref, bf16[8192,4096]{1,0:T(8,128)(2,1)} %bitcast.25.wm_ref.wr_ref, ...), custom_call_target="tpu_custom_call", output_to_operand_aliasing={{}: (7, {})} | custom-call | flops 17179869184 | bytes 67108864 | tf_op jit(solution)/shard_map/oproj/pallas_call | solution.py:181
  541.8 1.0 copy-done.8
  542.7 0.9 copy-done.9
  543.7 72.9 %qkva.5 = (bf16[256,4096]{1,0:T(8,128)(2,1)}, bf16[256,4096]{1,0:T(8,128)(2,1)}) custom-call(bf16[128,4096]{1,0:T(8,128)(2,1)} %collective-permute-done.13.refs_0_.rest_0_, bf16[128,4096]{1,0:T(8,128)(2,1)} %copy-done.7, bf16[128,4096]{1,0:T(8,128)(2,1)} %copy-done.8, bf16[128,4096]{1,0:T(8,128)(2,1)} %copy-done.9, f32[1,4096]{1,0:T(1,128)} %refs_4_.5, ...), custom_call_target="tpu_custom_call" | custom-call | flops 51539607552 | bytes 100663296 | tf_op jit(solution)/shard_map/qkva/pallas_call | solution.py:146
  617.1 4.0 collective-permute-done.23.ar_ref
  621.1 1.4 copy-done.5
  622.4 29.9 %oproj.5 = bf16[768,4096]{1,0:T(8,128)(2,1)} custom-call(s32[1]{0:T(128)} %bitcast.sp, bf16[256,4096]{1,0:T(8,128)(2,1)} %get-tuple-element.68.am_ref, bf16[256,4096]{1,0:T(8,128)(2,1)} %copy-done.5, bf16[8192,4096]{1,0:T(8,128)(2,1)} %bitcast.25.wm_ref.wr_ref, bf16[8192,4096]{1,0:T(8,128)(2,1)} %bitcast.25.wm_ref.wr_ref, ...), custom_call_target="tpu_custom_call", output_to_operand_aliasing={{}: (7, {})} | custom-call | flops 17179869184 | bytes 67108864 | tf_op jit(solution)/shard_map/oproj/pallas_call | solution.py:181
  (49 shorter events, 2.2 us)
Async XLA Ops:
  37.2 29.9 %collective-permute-start.1 = (f32[4,128,4096]{2,1,0:T(8,128)}, f32[4,128,4096]{2,1,0:T(8,128)}, u32[]{:S(2)}, u32[]{:S(2)}) collective-permute-start(f32[4,128,4096]{2,1,0:T(8,128)} %partials.7), channel_id=1, source_target_pairs={{0,1},{1,0},{2,3},{3,2},{4,5},{5,4},{6,7},{7,6}} | collective-permute-start | bytes 25165832 | tf_op jit(solution)/shard_map/ppermute | solution.py:223
  37.2 19.5 %collective-permute-start = (f32[2,128,4096]{2,1,0:T(8,128)}, f32[2,128,4096]{2,1,0:T(8,128)}, u32[]{:S(2)}, u32[]{:S(2)}) collective-permute-start(f32[2,128,4096]{2,1,0:T(8,128)} %partials.6), channel_id=1, source_target_pairs={{0,1},{1,0},{2,3},{3,2},{4,5},{5,4},{6,7},{7,6}} | collective-permute-start | bytes 12582920 | tf_op jit(solution)/shard_map/ppermute | solution.py:222
  103.5 35.0 %collective-permute-start.2 = (f32[6,128,4096]{2,1,0:T(8,128)}, f32[6,128,4096]{2,1,0:T(8,128)}, u32[]{:S(2)}, u32[]{:S(2)}) collective-permute-start(f32[6,128,4096]{2,1,0:T(8,128)} %partials.10), channel_id=1, source_target_pairs={{0,1},{1,0},{2,3},{3,2},{4,5},{5,4},{6,7},{7,6}} | collective-permute-start | bytes 37748744 | tf_op jit(solution)/shard_map/ppermute | solution.py:228
  103.7 66.9 %collective-permute-start.3 = (f32[1,128,4096]{2,1,0:T(8,128)}, f32[1,128,4096]{2,1,0:T(8,128)}, u32[]{:S(2)}, u32[]{:S(2)}) collective-permute-start(f32[1,128,4096]{2,1,0:T(8,128)} %get-tuple-element.41), channel_id=1, source_target_pairs={{0,2},{1,3},{2,0},{3,1},{4,6},{5,7},{6,4},{7,5}} | collective-permute-start | bytes 6291464 | tf_op jit(solution)/shard_map/ppermute | solution.py:225
  103.7 93.7 %collective-permute-start.5 = (f32[1,128,4096]{2,1,0:T(8,128)}, f32[1,128,4096]{2,1,0:T(8,128)}, u32[]{:S(2)}, u32[]{:S(2)}) collective-permute-start(f32[1,128,4096]{2,1,0:T(8,128)} %get-tuple-element.49), channel_id=1, source_target_pairs={{0,2},{1,3},{2,0},{3,1},{4,6},{5,7},{6,4},{7,5}} | collective-permute-start | bytes 6291464 | tf_op jit(solution)/shard_map/ppermute | solution.py:225
  105.7 163.1 %collective-permute-start.6 = (f32[1,128,4096]{2,1,0:T(8,128)}, f32[1,128,4096]{2,1,0:T(8,128)}, u32[]{:S(2)}, u32[]{:S(2)}) collective-permute-start(f32[1,128,4096]{2,1,0:T(8,128)} %get-tuple-element.43), channel_id=1, source_target_pairs={{0,2},{1,3},{2,0},{3,1},{4,6},{5,7},{6,4},{7,5}} | collective-permute-start | bytes 6291464 | tf_op jit(solution)/shard_map/ppermute | solution.py:227
  170.6 26.9 %copy-start.2 = (f32[128,4096]{1,0:T(8,128)S(1)}, f32[128,4096]{1,0:T(8,128)}, u32[]{:S(2)}) copy-start(f32[128,4096]{1,0:T(8,128)} %get-tuple-element.48) | copy-start | bytes 6291460
  200.7 67.6 %collective-permute-start.7 = (bf16[128,4096]{1,0:T(8,128)(2,1)}, bf16[128,4096]{1,0:T(8,128)(2,1)}, u32[]{:S(2)}, u32[]{:S(2)}) collective-permute-start(bf16[128,4096]{1,0:T(8,128)(2,1)} %fusion.3), channel_id=1, source_target_pairs={{0,4},{4,0},{1,5},{5,1},{2,6},{6,2},{3,7},{7,3}} | collective-permute-start | bytes 3145736 | tf_op jit(solution)/shard_map/ppermute | solution.py:240
  202.2 66.1 %collective-permute-start.4 = (bf16[128,4096]{1,0:T(8,128)(2,1)S(1)}, bf16[128,4096]{1,0:T(8,128)(2,1)}, u32[]{:S(2)}, u32[]{:S(2)}) collective-permute-start(bf16[128,4096]{1,0:T(8,128)(2,1)S(1)} %fusion.7), channel_id=1, source_target_pairs={{0,4},{4,0},{1,5},{5,1},{2,6},{6,2},{3,7},{7,3}} | collective-permute-start | bytes 3145736 | tf_op jit(solution)/shard_map/ppermute | solution.py:240
  202.7 143.9 %collective-permute-start.10 = (f32[1,128,4096]{2,1,0:T(8,128)}, f32[1,128,4096]{2,1,0:T(8,128)}, u32[]{:S(2)}, u32[]{:S(2)}) collective-permute-start(f32[1,128,4096]{2,1,0:T(8,128)} %get-tuple-element.56), channel_id=1, source_target_pairs={{0,2},{1,3},{2,0},{3,1},{4,6},{5,7},{6,4},{7,5}} | collective-permute-start | bytes 6291464 | tf_op jit(solution)/shard_map/ppermute | solution.py:227
  268.3 5.7 collective-permute-start.9
  268.3 5.7 collective-permute-start.8
  271.9 79.8 %collective-permute-start.14 = (bf16[128,4096]{1,0:T(8,128)(2,1)}, bf16[128,4096]{1,0:T(8,128)(2,1)S(1)}, u32[]{:S(2)}, u32[]{:S(2)}) collective-permute-start(bf16[128,4096]{1,0:T(8,128)(2,1)} %fusion.5), channel_id=1, source_target_pairs={{0,4},{4,0},{1,5},{5,1},{2,6},{6,2},{3,7},{7,3}} | collective-permute-start | bytes 3145736 | tf_op jit(solution)/shard_map/ppermute | solution.py:240
  346.6 27.9 %collective-permute-start.11 = (bf16[256,4096]{1,0:T(8,128)(2,1)}, bf16[256,4096]{1,0:T(8,128)(2,1)S(1)}, u32[]{:S(2)}, u32[]{:S(2)}) collective-permute-start(bf16[256,4096]{1,0:T(8,128)(2,1)} %get-tuple-element.58), channel_id=1, source_target_pairs={{0,1},{1,0},{2,3},{3,2},{4,5},{5,4},{6,7},{7,6}} | collective-permute-start | bytes 6291464 | tf_op jit(solution)/shard_map/ppermute | solution.py:248
  348.8 25.7 %collective-permute-start.15 = (bf16[128,4096]{1,0:T(8,128)(2,1)S(1)}, bf16[128,4096]{1,0:T(8,128)(2,1)}, u32[]{:S(2)}, u32[]{:S(2)}) collective-permute-start(bf16[128,4096]{1,0:T(8,128)(2,1)S(1)} %fusion.9), channel_id=1, source_target_pairs={{0,4},{4,0},{1,5},{5,1},{2,6},{6,2},{3,7},{7,3}} | collective-permute-start | bytes 3145736 | tf_op jit(solution)/shard_map/ppermute | solution.py:240
  349.8 56.3 %collective-permute-start.12 = (f32[1,128,4096]{2,1,0:T(8,128)}, f32[1,128,4096]{2,1,0:T(8,128)}, u32[]{:S(2)}, u32[]{:S(2)}) collective-permute-start(f32[1,128,4096]{2,1,0:T(8,128)} %get-tuple-element.60), channel_id=1, source_target_pairs={{0,2},{1,3},{2,0},{3,1},{4,6},{5,7},{6,4},{7,5}} | collective-permute-start | bytes 6291464 | tf_op jit(solution)/shard_map/ppermute | solution.py:227
  351.3 131.8 %collective-permute-start.18 = (f32[1,128,4096]{2,1,0:T(8,128)}, f32[1,128,4096]{2,1,0:T(8,128)}, u32[]{:S(2)}, u32[]{:S(2)}) collective-permute-start(f32[1,128,4096]{2,1,0:T(8,128)} %get-tuple-element.64), channel_id=1, source_target_pairs={{0,2},{1,3},{2,0},{3,1},{4,6},{5,7},{6,4},{7,5}} | collective-permute-start | bytes 6291464 | tf_op jit(solution)/shard_map/ppermute | solution.py:227
  351.8 54.2 %copy-start.6 = (bf16[128,4096]{1,0:T(8,128)(2,1)}, bf16[128,4096]{1,0:T(8,128)(2,1)S(1)}, u32[]{:S(2)}) copy-start(bf16[128,4096]{1,0:T(8,128)(2,1)S(1)} %collective-permute-done.14.refs_0_.rest_0_) | copy-start | bytes 3145732
  351.8 58.2 %collective-permute-start.16 = (bf16[128,4096]{1,0:T(8,128)(2,1)S(1)}, bf16[128,4096]{1,0:T(8,128)(2,1)}, u32[]{:S(2)}, u32[]{:S(2)}) collective-permute-start(bf16[128,4096]{1,0:T(8,128)(2,1)S(1)} %collective-permute-done.14.refs_0_.rest_0_), channel_id=1, source_target_pairs={{0,1},{1,0},{2,3},{3,2},{4,5},{5,4},{6,7},{7,6}} | collective-permute-start | bytes 3145736 | tf_op jit(solution)/shard_map/ppermute | solution.py:241
  374.5 35.5 %collective-permute-start.17 = (bf16[128,4096]{1,0:T(8,128)(2,1)}, bf16[128,4096]{1,0:T(8,128)(2,1)}, u32[]{:S(2)}, u32[]{:S(2)}) collective-permute-start(bf16[128,4096]{1,0:T(8,128)(2,1)} %collective-permute-done.15.refs_1_.rest_1_), channel_id=1, source_target_pairs={{0,1},{1,0},{2,3},{3,2},{4,5},{5,4},{6,7},{7,6}} | collective-permute-start | bytes 3145736 | tf_op jit(solution)/shard_map/ppermute | solution.py:241
  374.5 1.4 copy-start.3
  375.9 30.1 %copy-start.1 = (f32[128,4096]{1,0:T(8,128)S(1)}, f32[128,4096]{1,0:T(8,128)}, u32[]{:S(2)}) copy-start(f32[128,4096]{1,0:T(8,128)} %get-tuple-element.59) | copy-start | bytes 6291460
  409.2 73.8 %copy-start = (f32[128,4096]{1,0:T(8,128)S(1)}, f32[128,4096]{1,0:T(8,128)}, u32[]{:S(2)}) copy-start(f32[128,4096]{1,0:T(8,128)} %get-tuple-element.63) | copy-start | bytes 6291460
  409.2 77.2 %collective-permute-start.13 = (bf16[128,4096]{1,0:T(8,128)(2,1)}, bf16[128,4096]{1,0:T(8,128)(2,1)}, u32[]{:S(2)}, u32[]{:S(2)}) collective-permute-start(bf16[128,4096]{1,0:T(8,128)(2,1)} %fusion.11), channel_id=1, source_target_pairs={{0,4},{4,0},{1,5},{5,1},{2,6},{6,2},{3,7},{7,3}} | collective-permute-start | bytes 3145736 | tf_op jit(solution)/shard_map/ppermute | solution.py:240
  482.7 27.8 %collective-permute-start.19 = (bf16[256,4096]{1,0:T(8,128)(2,1)}, bf16[256,4096]{1,0:T(8,128)(2,1)S(1)}, u32[]{:S(2)}, u32[]{:S(2)}) collective-permute-start(bf16[256,4096]{1,0:T(8,128)(2,1)} %get-tuple-element.66), channel_id=1, source_target_pairs={{0,1},{1,0},{2,3},{3,2},{4,5},{5,4},{6,7},{7,6}} | collective-permute-start | bytes 6291464 | tf_op jit(solution)/shard_map/ppermute | solution.py:248
  485.3 25.3 %collective-permute-start.20 = (bf16[128,4096]{1,0:T(8,128)(2,1)S(1)}, bf16[128,4096]{1,0:T(8,128)(2,1)S(1)}, u32[]{:S(2)}, u32[]{:S(2)}) collective-permute-start(bf16[128,4096]{1,0:T(8,128)(2,1)S(1)} %fusion.1), channel_id=1, source_target_pairs={{0,4},{4,0},{1,5},{5,1},{2,6},{6,2},{3,7},{7,3}} | collective-permute-start | bytes 3145736 | tf_op jit(solution)/shard_map/ppermute | solution.py:240
  486.4 55.3 %collective-permute-start.21 = (bf16[128,4096]{1,0:T(8,128)(2,1)}, bf16[128,4096]{1,0:T(8,128)(2,1)S(1)}, u32[]{:S(2)}, u32[]{:S(2)}) collective-permute-start(bf16[128,4096]{1,0:T(8,128)(2,1)} %collective-permute-done.13.refs_0_.rest_0_), channel_id=1, source_target_pairs={{0,1},{1,0},{2,3},{3,2},{4,5},{5,4},{6,7},{7,6}} | collective-permute-start | bytes 3145736 | tf_op jit(solution)/shard_map/ppermute | solution.py:241
  510.5 31.2 %copy-start.7 = (bf16[128,4096]{1,0:T(8,128)(2,1)}, bf16[128,4096]{1,0:T(8,128)(2,1)S(1)}, u32[]{:S(2)}) copy-start(bf16[128,4096]{1,0:T(8,128)(2,1)S(1)} %collective-permute-done.20.refs_1_.rest_1_) | copy-start | bytes 3145732
  510.5 31.2 %collective-permute-start.22 = (bf16[128,4096]{1,0:T(8,128)(2,1)S(1)}, bf16[128,4096]{1,0:T(8,128)(2,1)S(1)}, u32[]{:S(2)}, u32[]{:S(2)}) collective-permute-start(bf16[128,4096]{1,0:T(8,128)(2,1)S(1)} %collective-permute-done.20.refs_1_.rest_1_), channel_id=1, source_target_pairs={{0,1},{1,0},{2,3},{3,2},{4,5},{5,4},{6,7},{7,6}} | collective-permute-start | bytes 3145736 | tf_op jit(solution)/shard_map/ppermute | solution.py:241
  510.5 1.3 copy-start.4
  541.8 1.0 copy-start.8
  542.7 0.9 copy-start.9
  616.6 4.5 collective-permute-start.23
  621.0 1.4 copy-start.5
